TPU v7x, 128 devices: a whole 4x4x4 slice. The times are simulated.
128 devices in a mesh: batch: 4 (over z), seq: 16 (over y, x_lo, core), head: 2 (over x_hi).
Axes of the slice: x: 4 (x_hi: 2, x_lo: 2; x = x_hi * 2 + x_lo), y: 4, z: 4, core: 2. Of those that a mesh axis runs over, the one named last changes fastest.
Arguments:
- image_hidden: bfloat16 [8, 4096, 3072], P('batch', 'seq', 'head'), parts along dimension 0, may hold values from -6 to 6
- modulation: float32 [8, 3, 3072], P('batch'), parts along dimension 0, may hold values from -4 to 4
- qkv_weight: bfloat16 [3072, 3, 1536], P(None, None, 'head'), may hold values from -0.109375 to 0.109375
- out_weight: bfloat16 [1536, 3072], P('head'), may hold values from -0.15625 to 0.15625
- q_gain: float32 [128], replicated, may hold values from 1.2 to 2.5
- k_gain: float32 [128], replicated, may hold values from 1.2 to 2.5
- text_keys: bfloat16 [8, 512, 1536], P('batch', 'seq', 'head'), parts along dimension 0, may hold values from -10 to 10
- text_values: bfloat16 [8, 512, 1536], P('batch', 'seq', 'head'), parts along dimension 0, may hold values from -6 to 6
- stale_keys: bfloat16 [8, 4096, 1536], P('batch', 'seq', 'head'), parts along dimension 0, may hold values from -64 to 64
- stale_values: bfloat16 [8, 4096, 1536], P('batch', 'seq', 'head'), parts along dimension 0, may hold values from -6 to 6
- cached_residual: bfloat16 [8, 4096, 3072], P('batch', 'seq', 'head'), parts along dimension 0, may hold values from -6 to 6
- patch_of: int32 [64], P('batch'), parts along dimension 0, may hold values from 0 to 15, each once
- refresh: int32 [64], P('batch'), parts along dimension 0, may hold values from 0 to 1, as said below
- text_len: int32 [8], P('batch'), parts along dimension 0, may hold values from 64 to 512
Outputs:
- image_out: bfloat16 [8, 4096, 3072], P('batch', 'seq', 'head'), parts along dimension 0
There are 4 independent parts, one for each index of `batch`. A program takes and returns all parts, laid end to end along the dimension named above; an argument that names none is the same for every part. Nothing has to cross between parts.
Inputs may be any that keep to these rules, and one draw needn't show every extreme that they name: `patch_of`: A permutation: every image band sits on exactly one index of seq. `refresh`: exactly 4 entries are 1, the rest 0.
All inputs are finite; a program needn't handle non-finite values.
Results may differ from a plain program's by a relative error of at most 0.012.
The roundings to bfloat16 on the way count: a program that leaves them out, or rounds other values in their place, can miss the bound.
Values may be sent and summed in bfloat16 or wider, within the bound.
No kernel may reach another device: no remote copies, remote signals or barrier semaphores. Data moves between devices by JAX's collectives and lax.ppermute only.
A program may use at most 192 MiB of HBM per device.

v0:
```python
import jax
import jax.numpy as jnp
from jax import lax
from jax.experimental import pallas as pl
from jax.experimental.pallas import tpu as pltpu
from jax.sharding import PartitionSpec as P


GRID_W = 64
EPS = 1e-06
LOG2E = 1.4426950408889634
F32 = jnp.float32
BF16 = jnp.bfloat16
NEG = -1e30
VMEM = 56 * 1024 * 1024
SLOTS = 8


def rotary_tables(raster, head_dim, grid_width):
    half_dim = head_dim // 2
    first_pairs = head_dim // 16
    axis_pairs = (half_dim - first_pairs) // 2
    pair_index = jnp.arange(half_dim, dtype=jnp.int32)
    pair_local = jnp.where(
        pair_index < first_pairs + axis_pairs,
        pair_index - first_pairs,
        pair_index - first_pairs - axis_pairs,
    )
    exponent = -pair_local.astype(F32) / float(axis_pairs)
    frequency = jnp.where(pair_index < first_pairs, F32(0.0), jnp.power(F32(10000.0), exponent))
    row_pos = (raster // grid_width).astype(F32)
    col_pos = (raster % grid_width).astype(F32)
    position = jnp.where(
        pair_index[None, :] < first_pairs + axis_pairs, row_pos[:, None], col_pos[:, None]
    )
    angles = position * frequency[None, :]
    cosine = jnp.cos(angles)
    sine = jnp.sin(angles)
    return (jnp.concatenate([cosine, cosine], axis=-1), jnp.concatenate([-sine, sine], axis=-1))


def qkv_body(
    info, own, oth, mod_own, mod_oth, w_own, w_oth, gains, cos, sin, stale_k, stale_v, send, fresh, mod_s
):
    n = pl.program_id(0)
    prompts, rows, part = own.shape
    width = 2 * part
    tile = 16

    @pl.when(n == 0)
    def _():
        for p in range(prompts):
            def norm(i, c):
                at = pl.multiple_of(i * tile, tile)
                a = own[p, pl.ds(at, tile), :].astype(F32)
                b = oth[p, pl.ds(at, tile), :].astype(F32)
                mean = (jnp.sum(a, -1, keepdims=True) + jnp.sum(b, -1, keepdims=True)) / width
                a, b = a - mean, b - mean
                var = (jnp.sum(a * a, -1, keepdims=True) + jnp.sum(b * b, -1, keepdims=True)) / width
                inv = lax.rsqrt(var + EPS)
                a = a * inv * (1.0 + mod_own[1, p : p + 1, :]) + mod_own[0, p : p + 1, :]
                b = b * inv * (1.0 + mod_oth[1, p : p + 1, :]) + mod_oth[0, p : p + 1, :]
                to = pl.multiple_of(p * rows + i * tile, tile)
                mod_s[pl.ds(to, tile), 0:part] = a.astype(BF16)
                mod_s[pl.ds(to, tile), part:width] = b.astype(BF16)
                return c

            lax.fori_loop(0, rows // tile, norm, 0, unroll=4)

    heads = w_own.shape[2] // 128
    per = 2
    flag = info[1]

    def products():
        for j in range(0, heads, per):
            cols = slice(j * 128, (j + per) * 128)
            acc = jnp.dot(mod_s[:, 0:part], w_own[0, :, cols], preferred_element_type=F32)
            acc = acc + jnp.dot(mod_s[:, part:width], w_oth[0, :, cols], preferred_element_type=F32)
            for p in range(prompts):
                for e in range(per):
                    yield p, j + e, acc[p * rows : (p + 1) * rows, e * 128 : (e + 1) * 128]

    def turned(x, gain):
        x = x * lax.rsqrt(jnp.mean(x * x, axis=-1, keepdims=True) + EPS) * gain
        return x * cos[...] + pltpu.roll(x, 64, 1) * sin[...]

    @pl.when(n == 0)
    def _():
        for p, j, x in products():
            send[p, j, 0] = turned(x, gains[0:1, :]).astype(BF16)

    @pl.when(n == 1)
    def _():
        for p, j, x in products():
            new = turned(x, gains[1:2, :]).astype(BF16)
            fresh[p, j, 0] = new
            send[p, j, 0] = jnp.where(flag == 1, new, stale_k[p, :, j * 128 : (j + 1) * 128])

    @pl.when(n == 2)
    def _():
        for p, j, x in products():
            new = x.astype(BF16)
            fresh[p, j, 0] = new
            send[p, j, 0] = jnp.where(flag == 1, new, stale_v[p, :, j * 128 : (j + 1) * 128])


def qkv(info, own, oth, modulation, w, gains, cos, sin, stale_k, stale_v):
    prompts, rows, part = own.shape
    channels = stale_k.shape[2]
    heads = channels // 128
    whole = lambda *shape: pl.BlockSpec(shape, lambda n, s: (0,) * len(shape))
    return pl.pallas_call(
        qkv_body,
        grid_spec=pltpu.PrefetchScalarGridSpec(
            num_scalar_prefetch=1,
            grid=(3,),
            in_specs=[
                whole(prompts, rows, part),
                whole(prompts, rows, part),
                pl.BlockSpec((3, prompts, part), lambda n, s: (0, 0, s[0])),
                pl.BlockSpec((3, prompts, part), lambda n, s: (0, 0, 1 - s[0])),
                pl.BlockSpec((1, part, channels), lambda n, s: (n, s[0], 0)),
                pl.BlockSpec((1, part, channels), lambda n, s: (n, 1 - s[0], 0)),
                whole(2, 128),
                whole(rows, 128),
                whole(rows, 128),
                whole(prompts, rows, channels),
                whole(prompts, rows, channels),
            ],
            out_specs=[
                pl.BlockSpec((prompts, SLOTS, 1, rows, 128), lambda n, s: (0, 0, n, 0, 0)),
                pl.BlockSpec(
                    (prompts, heads, 1, rows, 128), lambda n, s: (0, 0, jnp.maximum(n - 1, 0), 0, 0)
                ),
            ],
            scratch_shapes=[pltpu.VMEM((prompts * rows, 2 * part), BF16)],
        ),
        out_shape=[
            jax.ShapeDtypeStruct((prompts, SLOTS, 3, rows, 128), BF16),
            jax.ShapeDtypeStruct((prompts, heads, 2, rows, 128), BF16),
        ],
        compiler_params=pltpu.CompilerParams(
            dimension_semantics=("arbitrary",), vmem_limit_bytes=VMEM
        ),
        cost_estimate=pl.CostEstimate(
            flops=2 * prompts * rows * 2 * part * 3 * channels, bytes_accessed=20_000_000, transcendentals=0
        ),
        name="qkv",
    )(info, own, oth, modulation, modulation, w, w, gains, cos, sin, stale_k, stale_v)


def diag_body(q, kv, out):
    c = 128**-0.5 * LOG2E
    rows = q.shape[3]
    for e in range(q.shape[1]):
        s = lax.dot_general(q[0, e, 0], kv[0, e, 0], (((1,), (1,)), ((), ())), preferred_element_type=F32) * c
        top = jnp.max(s, axis=-1, keepdims=True)
        w = jnp.exp2(s - top)
        total = jnp.sum(w, axis=-1, keepdims=True)
        o = jnp.dot(w.astype(BF16), kv[0, e, 1], preferred_element_type=F32)
        out[0, e, 0:rows, :] = (o / total).astype(BF16)
        lse = jnp.transpose(jnp.broadcast_to(top + jnp.log2(total), (rows, 128)))[0:8, :]
        first = lse.astype(BF16).astype(F32)
        second = (lse - first).astype(BF16).astype(F32)
        third = lse - first - second
        at = lax.broadcasted_iota(jnp.int32, lse.shape, 0)
        pieces = jnp.where(at == 0, first, jnp.where(at == 1, second, third))
        pieces = jnp.concatenate([pieces[:, i : i + 128] for i in range(0, rows, 128)], 0)
        out[0, e, rows : rows + rows // 16, :] = pieces.astype(BF16)


def diag(send, fresh):
    prompts, heads, _, rows, _ = fresh.shape
    tall = rows + rows // 16
    per = heads
    return pl.pallas_call(
        diag_body,
        grid=(prompts,),
        in_specs=[
            pl.BlockSpec((1, per, 1, rows, 128), lambda p: (p, 0, 0, 0, 0)),
            pl.BlockSpec((1, per, 2, rows, 128), lambda p: (p, 0, 0, 0, 0)),
        ],
        out_specs=pl.BlockSpec((1, SLOTS, tall, 128), lambda p: (p, 0, 0, 0)),
        out_shape=jax.ShapeDtypeStruct((prompts, SLOTS, tall, 128), BF16),
        compiler_params=pltpu.CompilerParams(
            dimension_semantics=("arbitrary",), vmem_limit_bytes=VMEM
        ),
        cost_estimate=pl.CostEstimate(
            flops=4 * prompts * heads * rows * rows * 128,
            bytes_accessed=4_000_000,
            transcendentals=prompts * heads * rows * rows,
        ),
        name="diag",
    )(send, fresh)


def attend_body(info, got, text, out, stat, s_even, s_odd, top_s):
    g = pl.program_id(0)
    blocks, _, rows, _ = got.shape
    c = 128**-0.5 * LOG2E
    txt = text.shape[1]
    lead = txt // rows
    tiles = lead + blocks - 1
    contract = (((1,), (1,)), ((), ()))

    def keys(b, i, which):
        if i < lead:
            return text[which, i * rows : (i + 1) * rows, :]
        return got[lax.rem(b + 1 + (i - lead), blocks), 1 + which]

    def score(b, i, top, s_ref):
        s = lax.dot_general(got[b, 0], keys(b, i, 0), contract, preferred_element_type=F32)
        if i < lead:
            at = i * rows + lax.broadcasted_iota(jnp.int32, s.shape, 1)
            s = jnp.where(at < info[0], s, NEG)
        s_ref[i] = s
        for e in range(rows // 128):
            part = s[:, e * 128 : (e + 1) * 128]
            top = part if top is None else jnp.maximum(top, part)
        return top

    def lane_top(top):
        return jnp.broadcast_to(jnp.max(top, axis=-1, keepdims=True) * c, (rows, 128))

    @pl.when(g == 0)
    def _():
        top = None
        for i in range(tiles):
            top = score(0, i, top, s_even)
        top_s[...] = lane_top(top)

    top = top_s[...]
    for k in range(2):
        b = 2 * g + k
        nxt = lax.rem(b + 1, blocks)
        here, there = (s_even, s_odd) if k == 0 else (s_odd, s_even)
        total = None
        acc = None
        nxt_top = None
        for i in range(tiles):
            nxt_top = score(nxt, i, nxt_top, there)
            s = here[i]
            w = []
            for e in range(rows // 128):
                part = jnp.exp2(s[:, e * 128 : (e + 1) * 128] * c - top)
                total = part if total is None else total + part
                w.append(part.astype(BF16))
            o = jnp.dot(jnp.concatenate(w, 1), keys(b, i, 1), preferred_element_type=F32)
            acc = o if acc is None else acc + o
        total = jnp.sum(total, axis=-1, keepdims=True)
        out[k] = acc
        lane = lax.broadcasted_iota(jnp.int32, (rows, 128), 1)
        stat[k] = jnp.where(lane < 64, top, total)
        top = lane_top(nxt_top)
    top_s[...] = top


def attend(info, got, text):
    blocks, _, rows, _ = got.shape
    txt = text.shape[1]
    tiles = txt // rows + blocks - 1
    return pl.pallas_call(
        attend_body,
        grid_spec=pltpu.PrefetchScalarGridSpec(
            num_scalar_prefetch=1,
            grid=(blocks // 2,),
            in_specs=[
                pl.BlockSpec(got.shape, lambda b, s: (0, 0, 0, 0)),
                pl.BlockSpec(text.shape, lambda b, s: (0, 0, 0)),
            ],
            out_specs=[
                pl.BlockSpec((2, rows, 128), lambda b, s: (b, 0, 0)),
                pl.BlockSpec((2, rows, 128), lambda b, s: (b, 0, 0)),
            ],
            scratch_shapes=[
                pltpu.VMEM((tiles, rows, rows), F32),
                pltpu.VMEM((tiles, rows, rows), F32),
                pltpu.VMEM((rows, 128), F32),
            ],
        ),
        out_shape=[
            jax.ShapeDtypeStruct((blocks, rows, 128), F32),
            jax.ShapeDtypeStruct((blocks, rows, 128), F32),
        ],
        compiler_params=pltpu.CompilerParams(
            dimension_semantics=("arbitrary",), vmem_limit_bytes=VMEM
        ),
        cost_estimate=pl.CostEstimate(
            flops=4 * blocks * rows * tiles * rows * 128 * 2,
            bytes_accessed=8_000_000,
            transcendentals=blocks * rows * tiles * rows,
        ),
        name="attend",
    )(info, got, text)


def join_body(acc, stat, own, out):
    rows = acc.shape[1]
    for e in range(acc.shape[0]):
        top = stat[e, :, 0:1]
        total = stat[e, :, 64:65]
        pieces = own[e, rows : rows + rows // 16, :].astype(F32)
        other = []
        for i in range(0, rows // 16, 8):
            lse = pieces[i : i + 1] + pieces[i + 1 : i + 2] + pieces[i + 2 : i + 3]
            other.append(jnp.transpose(jnp.broadcast_to(lse, (128, 128))))
        other = jnp.concatenate(other, 0)
        high = jnp.maximum(other, top)
        u = jnp.exp2(top - high)
        w = jnp.exp2(other - high)
        o = (acc[e] * u + own[e, 0:rows, :].astype(F32) * w) / (total * u + w)
        o = o.astype(BF16)
        out[e, 0] = o
        out[e, 1] = o


def join(acc, stat, own):
    blocks, rows, _ = acc.shape
    per = 4
    return pl.pallas_call(
        join_body,
        grid=(blocks // per,),
        in_specs=[
            pl.BlockSpec((per, rows, 128), lambda b: (b, 0, 0)),
            pl.BlockSpec((per, rows, 128), lambda b: (b, 0, 0)),
            pl.BlockSpec((per, own.shape[1], 128), lambda b: (b, 0, 0)),
        ],
        out_specs=pl.BlockSpec((per, 2, rows, 128), lambda b: (b, 0, 0, 0)),
        out_shape=jax.ShapeDtypeStruct((blocks, 2, rows, 128), BF16),
        compiler_params=pltpu.CompilerParams(
            dimension_semantics=("arbitrary",), vmem_limit_bytes=VMEM
        ),
        name="join",
    )(acc, stat, own)


def project_body(info, got, w_own, w_oth, gate, hidden, cached, out, all_s):
    n = pl.program_id(0)
    prompts, rows, _ = hidden.shape
    part = w_own.shape[0]
    heads = part // 128
    h = info[0]

    @pl.when(n == 0)
    def _():
        for p in range(prompts):
            for k in range(2):
                seat = h if k == 0 else 1 - h
                for j in range(heads):
                    all_s[p * rows : (p + 1) * rows, (k * heads + j) * 128 : (k * heads + j + 1) * 128] = got[
                        (p * SLOTS + j) * 2 + seat
                    ]

    acc = jnp.dot(all_s[:, 0:part], w_own[...], preferred_element_type=F32)
    acc = acc + jnp.dot(all_s[:, part : 2 * part], w_oth[...], preferred_element_type=F32)
    for p in range(prompts):
        y = hidden[p].astype(F32) + gate[p] * acc[p * rows : (p + 1) * rows, :]
        out[p] = (y + cached[p].astype(F32)).astype(BF16)


def project(info, got, w_out, w_oth, gate, hidden, cached):
    prompts, rows, width = hidden.shape
    part = w_out.shape[0]
    bn = 512
    steps = width // bn
    return pl.pallas_call(
        project_body,
        grid_spec=pltpu.PrefetchScalarGridSpec(
            num_scalar_prefetch=1,
            grid=(steps,),
            in_specs=[
                pl.BlockSpec(got.shape, lambda n, s: (0, 0, 0)),
                pl.BlockSpec((part, bn), lambda n, s: (0, s[0] * steps + n)),
                pl.BlockSpec((part, bn), lambda n, s: (0, n)),
                pl.BlockSpec((prompts, 1, bn), lambda n, s: (0, 0, n)),
                pl.BlockSpec((prompts, rows, bn), lambda n, s: (0, 0, n)),
                pl.BlockSpec((prompts, rows, bn), lambda n, s: (0, 0, n)),
            ],
            out_specs=pl.BlockSpec((prompts, rows, bn), lambda n, s: (0, 0, n)),
            scratch_shapes=[pltpu.VMEM((prompts * rows, 2 * part), BF16)],
        ),
        out_shape=jax.ShapeDtypeStruct((prompts, rows, width), BF16),
        compiler_params=pltpu.CompilerParams(
            dimension_semantics=("arbitrary",), vmem_limit_bytes=VMEM
        ),
        cost_estimate=pl.CostEstimate(
            flops=4 * prompts * rows * part * width, bytes_accessed=12_000_000, transcendentals=0
        ),
        name="project",
    )(info, got, w_out, w_oth, gate, hidden, cached)


def per_device(
    image_hidden,
    modulation,
    qkv_weight,
    out_weight,
    q_gain,
    k_gain,
    text_keys,
    text_values,
    stale_keys,
    stale_values,
    cached_residual,
    patch_of,
    refresh,
    text_len,
):
    prompts, rows, width_part = image_hidden.shape
    head_dim = q_gain.shape[0]
    channels = out_weight.shape[0]
    heads = channels // head_dim
    seat = lax.axis_index("seq")
    head_seat = lax.axis_index("head")
    batch_seat = lax.axis_index("batch")
    n_seq = lax.axis_size("seq")
    n_batch = lax.axis_size("batch")
    swap = [(0, 1), (1, 0)]

    other_hidden = lax.ppermute(image_hidden, "head", swap)

    text = jnp.stack([text_keys, text_values], 1)
    t_rows = text.shape[2]
    text = text.reshape(prompts, 2, t_rows, heads, head_dim).transpose(0, 3, 1, 2, 4)
    text = jnp.pad(text, ((0, 0), (0, SLOTS - heads), (0, 0), (0, 0), (0, 0)))
    text = text.reshape(n_seq, 2, t_rows, head_dim)
    text = lax.all_to_all(text, "seq", split_axis=0, concat_axis=0, tiled=True)
    text = text.transpose(1, 0, 2, 3).reshape(2, n_seq * t_rows, head_dim)

    n_y = n_seq // 4
    y_seat = seat // 4
    share = channels // (n_batch * n_y)
    piece = lax.dynamic_slice(
        out_weight,
        ((batch_seat * n_y + y_seat) * share, (1 - head_seat) * width_part),
        (share, width_part),
    )
    piece = lax.ppermute(piece, "head", swap)
    w_y = jnp.zeros((n_y, share, width_part), BF16)
    w_y = lax.dynamic_update_slice(w_y, piece[None], (y_seat, 0, 0))
    for d in range(1, n_y):
        moved = lax.ppermute(piece, "seq", [(i, (i + 4 * d) % n_seq) for i in range(n_seq)])
        w_y = lax.dynamic_update_slice(w_y, moved[None], ((y_seat - d) % n_y, 0, 0))
    w_oth = jnp.zeros((n_batch, n_y, share, width_part), BF16)
    w_oth = lax.dynamic_update_slice(w_oth, w_y[None], (batch_seat, 0, 0, 0))
    for d in range(1, n_batch):
        moved = lax.ppermute(w_y, "batch", [(i, (i + d) % n_batch) for i in range(n_batch)])
        w_oth = lax.dynamic_update_slice(w_oth, moved[None], ((batch_seat - d) % n_batch, 0, 0, 0))
    w_oth = w_oth.reshape(channels, width_part)
    other_hidden, w_oth = lax.optimization_barrier((other_hidden, w_oth))

    seats = jnp.arange(n_seq, dtype=jnp.int32)
    own_band = jnp.sum(jnp.where(seats == seat, patch_of, 0))
    own_flag = jnp.sum(jnp.where(seats == seat, refresh, 0))
    raster = own_band * rows + jnp.arange(rows, dtype=jnp.int32)
    cos, sin = rotary_tables(raster, head_dim, GRID_W)
    info = jnp.stack([head_seat.astype(jnp.int32), own_flag.astype(jnp.int32)])
    send, fresh = qkv(
        info,
        image_hidden,
        other_hidden,
        modulation.transpose(1, 0, 2),
        qkv_weight.transpose(1, 0, 2),
        jnp.stack([q_gain, k_gain]),
        cos,
        sin,
        stale_keys,
        stale_values,
    )
    got = lax.all_to_all(
        send.reshape(n_seq, 3, rows, head_dim), "seq", split_axis=0, concat_axis=0, tiled=True
    )
    own_part = diag(send, fresh)
    unit_prompt = jnp.minimum(seat // SLOTS, prompts - 1)
    length = jnp.sum(jnp.where(jnp.arange(prompts) == unit_prompt, text_len, 0)).astype(jnp.int32)
    acc, stat = attend(length[None], got, text)
    own_part = lax.all_to_all(
        own_part.reshape(n_seq, -1, head_dim), "seq", split_axis=0, concat_axis=0, tiled=True
    )
    back = join(acc, stat, own_part)
    back = lax.all_to_all(
        back.reshape(n_seq * 2, rows, head_dim), ("seq", "head"), split_axis=0, concat_axis=0, tiled=True
    )
    gate = lax.dynamic_slice_in_dim(modulation[:, 2:3], head_seat * width_part, width_part, 2)
    return project(info, back, out_weight, w_oth, gate, image_hidden, cached_residual)


def solution(mesh):
    in_specs = (
        P("batch", "seq", "head"),
        P("batch", None, None),
        P(None, None, "head"),
        P("head", None),
        P(),
        P(),
        P("batch", "seq", "head"),
        P("batch", "seq", "head"),
        P("batch", "seq", "head"),
        P("batch", "seq", "head"),
        P("batch", "seq", "head"),
        P("batch"),
        P("batch"),
        P("batch"),
    )
    out_specs = P("batch", "seq", "head")
    return jax.shard_map(
        per_device, mesh=mesh, in_specs=in_specs, out_specs=out_specs, check_vma=False
    )
```

profile of v0, /device:TPU:0, one launch (start us, length us, event | category | flops | bytes accessed | tf_op | source)
XLA Modules:
  0.0 212.7 jit_solution(9945931553005167856)
XLA Ops:
  0.0 1.0 dynamic_slice.6
  1.0 3.2 %collective-permute-start.1 = (bf16[48,1536]{1,0:T(8,128)(2,1)S(1)}, bf16[48,1536]{1,0:T(8,128)(2,1)S(1)}, u32[]{:S(2)}, u32[]{:S(2)}) collective-permute-start(bf16[48,1536]{1,0:T(8,128)(2,1)S(1)} %dynamic_slice.6), channel_id=1, source_target_pairs={{0,1},{1,0},{2,3},{3,2},{4,5},{5,4},{6,7},{7,6},{8,9},{9,8},{10,11... | collective-permute-start | bytes 442376 | tf_op jit(solution)/shard_map/ppermute | solution.py:438
  4.2 0.4 collective-permute-start
  4.6 1.0 stack.33
  5.6 1.0 stack.34
  6.7 0.1 maximum_bitcast_fusion
  6.8 0.7 pad.4.clone
  7.5 5.6 %all-to-all-start.1 = ((bf16[16,2,32,128]{3,2,1,0:T(8,128)(2,1)}), bf16[16,2,32,128]{3,2,1,0:T(8,128)(2,1)S(1)}, u32[]{:S(2)}, u32[]{:S(2)}) async-start(bf16[16,2,32,128]{3,2,1,0:T(8,128)(2,1)} %bitcast.18), calls=%async_computation.1 | async-start | bytes 524288 | tf_op jit(solution)/shard_map/all_to_all | solution.py:427
  13.1 0.6 fusion.12
  14.4 0.5 fusion.2
  15.0 0.7 pad_maximum_fusion.cos
  15.7 0.6 fusion.11
  16.4 0.5 pad_maximum_fusion.2.gains
  16.9 0.8 pad_maximum_fusion.1.sin
  17.7 0.0 collective-permute-done.1
  17.7 1.9 collective-permute-start.2
  19.6 2.7 %collective-permute-start.3 = (bf16[48,1536]{1,0:T(8,128)(2,1)S(1)}, bf16[48,1536]{1,0:T(8,128)(2,1)S(1)}, u32[]{:S(2)}, u32[]{:S(2)}) collective-permute-start(bf16[48,1536]{1,0:T(8,128)(2,1)S(1)} %collective-permute-done.1), channel_id=1, source_target_pairs={{0,16},{2,18},{4,20},{6,22},{8,24},{10,26},{12,28},{14,30},{16,0},... | collective-permute-start | bytes 442376 | tf_op jit(solution)/shard_map/ppermute | solution.py:442
  22.3 1.5 collective-permute-start.4
  23.8 1.2 collective-permute-done.2
  25.1 4.2 %collective-permute-done.3 = bf16[48,1536]{1,0:T(8,128)(2,1)S(1)} collective-permute-done((bf16[48,1536]{1,0:T(8,128)(2,1)S(1)}, bf16[48,1536]{1,0:T(8,128)(2,1)S(1)}, u32[]{:S(2)}, u32[]{:S(2)}) %collective-permute-start.3) | collective-permute-done | bytes 147488 | tf_op jit(solution)/shard_map/ppermute | solution.py:442
  29.3 2.0 collective-permute-start.5
  31.3 1.3 pad_add_fusion.info
  32.6 3.6 %collective-permute-start.6 = (bf16[4,48,1536]{2,1,0:T(8,128)(2,1)S(1)}, bf16[4,48,1536]{2,1,0:T(8,128)(2,1)S(1)}, u32[]{:S(2)}, u32[]{:S(2)}) collective-permute-start(bf16[4,48,1536]{2,1,0:T(8,128)(2,1)S(1)} %bitcast_dynamic-update-slice_fusion.4), channel_id=1, source_target_pairs={{0,64},{32,96},{64,0},{96,32},{1,65},{33,97},{65,1},{97,33},{2,66}... | collective-permute-start | bytes 1769480 | tf_op jit(solution)/shard_map/ppermute | solution.py:447
  36.2 1.0 collective-permute-start.7
  37.2 0.2 broadcast_in_dim.77
  37.5 9.2 %collective-permute-done.5 = bf16[4,48,1536]{2,1,0:T(8,128)(2,1)S(1)} collective-permute-done((bf16[4,48,1536]{2,1,0:T(8,128)(2,1)S(1)}, bf16[4,48,1536]{2,1,0:T(8,128)(2,1)S(1)}, u32[]{:S(2)}, u32[]{:S(2)}) %collective-permute-start.5) | collective-permute-done | bytes 589856 | tf_op jit(solution)/shard_map/ppermute | solution.py:447
  46.8 13.3 %collective-permute-done.6 = bf16[4,48,1536]{2,1,0:T(8,128)(2,1)S(1)} collective-permute-done((bf16[4,48,1536]{2,1,0:T(8,128)(2,1)S(1)}, bf16[4,48,1536]{2,1,0:T(8,128)(2,1)S(1)}, u32[]{:S(2)}, u32[]{:S(2)}) %collective-permute-start.6) | collective-permute-done | bytes 589856 | tf_op jit(solution)/shard_map/ppermute | solution.py:447
  60.2 0.7 collective-permute-done.7
  60.9 18.7 %qkv.1 = (bf16[2,8,3,256,128]{4,3,2,1,0:T(8,128)(2,1)}, bf16[2,6,2,256,128]{4,3,2,1,0:T(8,128)(2,1)}) custom-call(s32[2]{0:T(128)} %pad_add_fusion.info, bf16[2,256,1536]{2,1,0:T(8,128)(2,1)} %hidden.1, bf16[2,256,1536]{2,1,0:T(8,128)(2,1)} %collective-permute-done.oth, f32[3,2,3072]{2,1,0:T(2,128)} %bitcast.39, f32[3,2,3072]{2,1,0:T(2,128)} %bitcast.40, ...), custom_call_target="tpu_custom_call" | custom-call | flops 7247757312 | bytes 20000000 | tf_op jit(solution)/shard_map/qkv/pallas_call | solution.py:112
  79.7 0.0 all-to-all-done.1
  79.7 0.0 copy-start.8
  79.7 4.8 %all-to-all-start = ((bf16[16,3,256,128]{3,2,1,0:T(8,128)(2,1)}), bf16[16,3,256,128]{3,2,1,0:T(8,128)(2,1)S(1)}, u32[]{:S(2)}, u32[]{:S(2)}) async-start(bf16[16,3,256,128]{3,2,1,0:T(8,128)(2,1)} %bitcast.34), calls=%async_computation | async-start | bytes 6291456 | tf_op jit(solution)/shard_map/all_to_all | solution.py:470
  84.5 0.7 fusion.13
  85.2 0.7 copy.19
  85.9 4.6 %diag.1 = bf16[2,8,272,128]{3,2,1,0:T(8,128)(2,1)} custom-call(bf16[2,8,3,256,128]{4,3,2,1,0:T(8,128)(2,1)} %get-tuple-element.12.q, bf16[2,6,2,256,128]{4,3,2,1,0:T(8,128)(2,1)} %get-tuple-element.15.kv), custom_call_target="tpu_custom_call" | custom-call | flops 402653184 | bytes 4000000 | tf_op jit(solution)/shard_map/diag/pallas_call | solution.py:176
  90.5 33.1 %all-to-all-done.got = bf16[16,3,256,128]{3,2,1,0:T(8,128)(2,1)S(1)} async-done(((bf16[16,3,256,128]{3,2,1,0:T(8,128)(2,1)}), bf16[16,3,256,128]{3,2,1,0:T(8,128)(2,1)S(1)}, u32[]{:S(2)}, u32[]{:S(2)}) %all-to-all-start) | async-done | bytes 3145760 | tf_op jit(solution)/shard_map/all_to_all | solution.py:470
  123.5 1.7 copy-done.3
  125.2 3.9 %all-to-all-start.2 = ((bf16[16,272,128]{2,1,0:T(8,128)(2,1)}), bf16[16,272,128]{2,1,0:T(8,128)(2,1)S(1)}, u32[]{:S(2)}, u32[]{:S(2)}) async-start(bf16[16,272,128]{2,1,0:T(8,128)(2,1)} %bitcast.37), calls=%async_computation.2 | async-start | bytes 2228224 | tf_op jit(solution)/shard_map/all_to_all | solution.py:477
  129.1 32.2 %attend.1 = (f32[16,256,128]{2,1,0:T(8,128)}, f32[16,256,128]{2,1,0:T(8,128)}) custom-call(s32[1]{0:T(128)} %bitcast.2.info, bf16[16,3,256,128]{3,2,1,0:T(8,128)(2,1)} %copy-done.3, bf16[2,512,128]{2,1,0:T(8,128)(2,1)} %bitcast.41), custom_call_target="tpu_custom_call" | custom-call | flops 18253611008 | bytes 8000000 | tf_op jit(solution)/shard_map/attend/pallas_call | solution.py:262
  161.3 0.0 all-to-all-done.2.own
  161.3 1.0 copy-done.2
  162.3 5.3 %join.1 = bf16[16,2,256,128]{3,2,1,0:T(8,128)(2,1)} custom-call(f32[16,256,128]{2,1,0:T(8,128)} %get-tuple-element.13.acc, f32[16,256,128]{2,1,0:T(8,128)} %get-tuple-element.14.stat, bf16[16,272,128]{2,1,0:T(8,128)(2,1)} %copy-done.2), custom_call_target="tpu_custom_call" | custom-call | tf_op jit(solution)/shard_map/join/pallas_call | solution.py:320
  167.6 7.1 %all-to-all-start.3 = ((bf16[32,256,128]{2,1,0:T(8,128)(2,1)}), bf16[32,256,128]{2,1,0:T(8,128)(2,1)S(1)}, u32[]{:S(2)}, u32[]{:S(2)}) async-start(bf16[32,256,128]{2,1,0:T(8,128)(2,1)} %bitcast.36), calls=%async_computation.3 | async-start | bytes 4194304 | tf_op jit(solution)/shard_map/all_to_all | solution.py:481
  174.7 0.7 slice.3
  175.4 0.6 copy.21.gate
  176.0 26.8 %all-to-all-done.3.got = bf16[32,256,128]{2,1,0:T(8,128)(2,1)S(1)} async-done(((bf16[32,256,128]{2,1,0:T(8,128)(2,1)}), bf16[32,256,128]{2,1,0:T(8,128)(2,1)S(1)}, u32[]{:S(2)}, u32[]{:S(2)}) %all-to-all-start.3) | async-done | bytes 2097184 | tf_op jit(solution)/shard_map/all_to_all | solution.py:481
  202.8 1.3 copy-done.1
  204.2 8.5 %project.1 = bf16[2,256,1536]{2,1,0:T(8,128)(2,1)} custom-call(s32[2]{0:T(128)} %pad_add_fusion.info, bf16[32,256,128]{2,1,0:T(8,128)(2,1)} %copy-done.1, bf16[768,3072]{1,0:T(8,128)(2,1)} %w_own.1, bf16[768,1536]{1,0:T(8,128)(2,1)} %bitcast.35, f32[2,1,1536]{2,1,0:T(1,128)} %copy.21.gate, bf16[2,256,1536]{2,1,0:T(8,128)(2,1)} %hidden.1, ...), custom_call_target="tpu_custom_call" | custom-call | flops 2415919104 | bytes 12000000 | tf_op jit(solution)/shard_map/project/pallas_call | solution.py:366
  (30 shorter events, 0.4 us)
Async XLA Ops:
  0.0 13.1 %copy-start.6 = (s32[16]{0:T(128)S(1)}, s32[16]{0:T(128)}, u32[]{:S(2)}) copy-start(s32[16]{0:T(128)} %param.25) | copy-start | bytes 196
  0.0 15.7 %copy-start.7 = (s32[16]{0:T(128)S(1)}, s32[16]{0:T(128)}, u32[]{:S(2)}) copy-start(s32[16]{0:T(128)} %param.26) | copy-start | bytes 196
  0.0 16.4 %copy-start.5 = (f32[128]{0:T(128)S(1)}, f32[128]{0:T(128)}, u32[]{:S(2)}) copy-start(f32[128]{0:T(128)} %param.18) | copy-start | bytes 1540
  0.0 16.4 %copy-start.4 = (f32[128]{0:T(128)S(1)}, f32[128]{0:T(128)}, u32[]{:S(2)}) copy-start(f32[128]{0:T(128)} %param.19) | copy-start | bytes 1540
  1.0 16.7 %collective-permute-start.1 = (bf16[48,1536]{1,0:T(8,128)(2,1)S(1)}, bf16[48,1536]{1,0:T(8,128)(2,1)S(1)}, u32[]{:S(2)}, u32[]{:S(2)}) collective-permute-start(bf16[48,1536]{1,0:T(8,128)(2,1)S(1)} %dynamic_slice.6), channel_id=1, source_target_pairs={{0,1},{1,0},{2,3},{3,2},{4,5},{5,4},{6,7},{7,6},{8,9},{9,8},{10,11... | collective-permute-start | bytes 442376 | tf_op jit(solution)/shard_map/ppermute | solution.py:438
  4.2 56.7 %collective-permute-start = (bf16[2,256,1536]{2,1,0:T(8,128)(2,1)}, bf16[2,256,1536]{2,1,0:T(8,128)(2,1)}, u32[]{:S(2)}, u32[]{:S(2)}) collective-permute-start(bf16[2,256,1536]{2,1,0:T(8,128)(2,1)} %hidden.1), channel_id=1, source_target_pairs={{0,1},{1,0},{2,3},{3,2},{4,5},{5,4},{6,7},{7,6},{8,9},{9,8},{10,11... | collective-permute-start | bytes 4718600 | tf_op jit(solution)/shard_map/ppermute | solution.py:420
  7.5 72.2 %all-to-all-start.1 = ((bf16[16,2,32,128]{3,2,1,0:T(8,128)(2,1)}), bf16[16,2,32,128]{3,2,1,0:T(8,128)(2,1)S(1)}, u32[]{:S(2)}, u32[]{:S(2)}) async-start(bf16[16,2,32,128]{3,2,1,0:T(8,128)(2,1)} %bitcast.18), calls=%async_computation.1 | async-start | bytes 524288 | tf_op jit(solution)/shard_map/all_to_all | solution.py:427
  17.7 7.4 %collective-permute-start.2 = (bf16[48,1536]{1,0:T(8,128)(2,1)S(1)}, bf16[48,1536]{1,0:T(8,128)(2,1)S(1)}, u32[]{:S(2)}, u32[]{:S(2)}) collective-permute-start(bf16[48,1536]{1,0:T(8,128)(2,1)S(1)} %collective-permute-done.1), channel_id=1, source_target_pairs={{0,8},{2,10},{4,12},{6,14},{8,16},{10,18},{12,20},{14,22},{16,24},... | collective-permute-start | bytes 442376 | tf_op jit(solution)/shard_map/ppermute | solution.py:442
  19.6 9.7 %collective-permute-start.3 = (bf16[48,1536]{1,0:T(8,128)(2,1)S(1)}, bf16[48,1536]{1,0:T(8,128)(2,1)S(1)}, u32[]{:S(2)}, u32[]{:S(2)}) collective-permute-start(bf16[48,1536]{1,0:T(8,128)(2,1)S(1)} %collective-permute-done.1), channel_id=1, source_target_pairs={{0,16},{2,18},{4,20},{6,22},{8,24},{10,26},{12,28},{14,30},{16,0},... | collective-permute-start | bytes 442376 | tf_op jit(solution)/shard_map/ppermute | solution.py:442
  22.3 7.0 %collective-permute-start.4 = (bf16[48,1536]{1,0:T(8,128)(2,1)S(1)}, bf16[48,1536]{1,0:T(8,128)(2,1)S(1)}, u32[]{:S(2)}, u32[]{:S(2)}) collective-permute-start(bf16[48,1536]{1,0:T(8,128)(2,1)S(1)} %collective-permute-done.1), channel_id=1, source_target_pairs={{0,24},{2,26},{4,28},{6,30},{8,0},{10,2},{12,4},{14,6},{16,8},{18,... | collective-permute-start | bytes 442376 | tf_op jit(solution)/shard_map/ppermute | solution.py:442
  29.3 17.4 %collective-permute-start.5 = (bf16[4,48,1536]{2,1,0:T(8,128)(2,1)S(1)}, bf16[4,48,1536]{2,1,0:T(8,128)(2,1)S(1)}, u32[]{:S(2)}, u32[]{:S(2)}) collective-permute-start(bf16[4,48,1536]{2,1,0:T(8,128)(2,1)S(1)} %bitcast_dynamic-update-slice_fusion.4), channel_id=1, source_target_pairs={{0,32},{32,64},{64,96},{96,0},{1,33},{33,65},{65,97},{97,1},{2,34}... | collective-permute-start | bytes 1769480 | tf_op jit(solution)/shard_map/ppermute | solution.py:447
  32.6 27.5 %collective-permute-start.6 = (bf16[4,48,1536]{2,1,0:T(8,128)(2,1)S(1)}, bf16[4,48,1536]{2,1,0:T(8,128)(2,1)S(1)}, u32[]{:S(2)}, u32[]{:S(2)}) collective-permute-start(bf16[4,48,1536]{2,1,0:T(8,128)(2,1)S(1)} %bitcast_dynamic-update-slice_fusion.4), channel_id=1, source_target_pairs={{0,64},{32,96},{64,0},{96,32},{1,65},{33,97},{65,1},{97,33},{2,66}... | collective-permute-start | bytes 1769480 | tf_op jit(solution)/shard_map/ppermute | solution.py:447
  36.2 24.7 %collective-permute-start.7 = (bf16[4,48,1536]{2,1,0:T(8,128)(2,1)S(1)}, bf16[4,48,1536]{2,1,0:T(8,128)(2,1)S(1)}, u32[]{:S(2)}, u32[]{:S(2)}) collective-permute-start(bf16[4,48,1536]{2,1,0:T(8,128)(2,1)S(1)} %bitcast_dynamic-update-slice_fusion.4), channel_id=1, source_target_pairs={{0,96},{32,0},{64,32},{96,64},{1,97},{33,1},{65,33},{97,65},{2,98}... | collective-permute-start | bytes 1769480 | tf_op jit(solution)/shard_map/ppermute | solution.py:447
  60.9 18.8 %copy-start = (bf16[4,4,48,1536]{3,2,1,0:T(8,128)(2,1)}, bf16[4,4,48,1536]{3,2,1,0:T(8,128)(2,1)S(1)}, u32[]{:S(2)}) copy-start(bf16[4,4,48,1536]{3,2,1,0:T(8,128)(2,1)S(1)} %bitcast_dynamic-update-slice_fusion) | copy-start | bytes 7077892
  79.7 4.8 %copy-start.8 = (s32[2]{0:T(128)S(1)}, s32[2]{0:T(128)}, u32[]{:S(2)}) copy-start(s32[2]{0:T(128)} %param.27) | copy-start | bytes 28
  79.7 43.8 %all-to-all-start = ((bf16[16,3,256,128]{3,2,1,0:T(8,128)(2,1)}), bf16[16,3,256,128]{3,2,1,0:T(8,128)(2,1)S(1)}, u32[]{:S(2)}, u32[]{:S(2)}) async-start(bf16[16,3,256,128]{3,2,1,0:T(8,128)(2,1)} %bitcast.34), calls=%async_computation | async-start | bytes 6291456 | tf_op jit(solution)/shard_map/all_to_all | solution.py:470
  123.5 1.7 copy-start.3
  125.2 36.1 %all-to-all-start.2 = ((bf16[16,272,128]{2,1,0:T(8,128)(2,1)}), bf16[16,272,128]{2,1,0:T(8,128)(2,1)S(1)}, u32[]{:S(2)}, u32[]{:S(2)}) async-start(bf16[16,272,128]{2,1,0:T(8,128)(2,1)} %bitcast.37), calls=%async_computation.2 | async-start | bytes 2228224 | tf_op jit(solution)/shard_map/all_to_all | solution.py:477
  161.3 1.0 copy-start.2
  167.6 35.3 %all-to-all-start.3 = ((bf16[32,256,128]{2,1,0:T(8,128)(2,1)}), bf16[32,256,128]{2,1,0:T(8,128)(2,1)S(1)}, u32[]{:S(2)}, u32[]{:S(2)}) async-start(bf16[32,256,128]{2,1,0:T(8,128)(2,1)} %bitcast.36), calls=%async_computation.3 | async-start | bytes 4194304 | tf_op jit(solution)/shard_map/all_to_all | solution.py:481
  202.8 1.3 copy-start.1
where the time goes:
time: 213 us
  waiting for transfers between devices  88.6 us (42%)
  Pallas kernels  69.3 us (33%)
  starting transfers between devices  37.6 us (18%)
  local copies, waits for them, and re-layouts  10.4 us (5%)
  other arithmetic  5.9 us (3%)
    all_to_all x1, waiting for transfers between devices, per_device(): lax.all_to_all(send.reshape(n_seq, 3, rows, head_dim), 'seq', split_axis=...  33.1 us
    pallas_call x1, Pallas kernels, attend(): pl.pallas_call(attend_body, grid_spec=pltpu.PrefetchScalarGridSpec(num_sc...  32.2 us
    all_to_all x1, waiting for transfers between devices, per_device(): lax.all_to_all(back.reshape(n_seq * 2, rows, head_dim), ('seq', 'head'),...  26.8 us
    ppermute x3, waiting for transfers between devices, per_device(): lax.ppermute(w_y, 'batch', [(i, (i + d) % n_batch) for i in range(n_batch)])  23.3 us
    pallas_call x1, Pallas kernels, qkv(): pl.pallas_call(qkv_body, grid_spec=pltpu.PrefetchScalarGridSpec(num_scala...  18.7 us
    pallas_call x1, Pallas kernels, project(): pl.pallas_call(project_body, grid_spec=pltpu.PrefetchScalarGridSpec(num_s...  8.55 us
    all_to_all x1, starting transfers between devices, per_device(): lax.all_to_all(back.reshape(n_seq * 2, rows, head_dim), ('seq', 'head'),...  7.1 us
    ppermute x3, starting transfers between devices, per_device(): lax.ppermute(w_y, 'batch', [(i, (i + d) % n_batch) for i in range(n_batch)])  6.58 us
  transfers between devices with their start and end apart: 12, of which 7 were waited for; matrix products, arithmetic and copies ran while one was open for 5% of the time, Pallas kernels for 26%

commit v1 on v0

--- a/solution.py
+++ b/solution.py
@@ -12,7 +12,7 @@
 F32 = jnp.float32
 BF16 = jnp.bfloat16
 NEG = -1e30
-VMEM = 56 * 1024 * 1024
+MIB = 1024 * 1024
 SLOTS = 8
 
 
@@ -100,8 +100,10 @@
     def _():
         for p, j, x in products():
             new = x.astype(BF16)
-            fresh[p, j, 0] = new
-            send[p, j, 0] = jnp.where(flag == 1, new, stale_v[p, :, j * 128 : (j + 1) * 128])
+            used = jnp.where(flag == 1, new, stale_v[p, :, j * 128 : (j + 1) * 128])
+            for r in range(0, rows, 128):
+                fresh[p, j, 0, r : r + 128, :] = jnp.transpose(new[r : r + 128, :])
+                send[p, j, 0, r : r + 128, :] = jnp.transpose(used[r : r + 128, :])
 
 
 def qkv(info, own, oth, modulation, w, gains, cos, sin, stale_k, stale_v):
@@ -140,50 +142,54 @@
             jax.ShapeDtypeStruct((prompts, heads, 2, rows, 128), BF16),
         ],
         compiler_params=pltpu.CompilerParams(
-            dimension_semantics=("arbitrary",), vmem_limit_bytes=VMEM
+            dimension_semantics=("arbitrary",), vmem_limit_bytes=36 * MIB
         ),
         cost_estimate=pl.CostEstimate(
             flops=2 * prompts * rows * 2 * part * 3 * channels, bytes_accessed=20_000_000, transcendentals=0
         ),
         name="qkv",
     )(info, own, oth, modulation, modulation, w, w, gains, cos, sin, stale_k, stale_v)
+
+
+def side_by_side(ref, at):
+    rows = ref.shape[-2]
+    return jnp.concatenate([ref[(*at, slice(r, r + 128), slice(None))] for r in range(0, rows, 128)], 1)
+
+
+CONTRACT = (((1,), (1,)), ((), ()))
 
 
 def diag_body(q, kv, out):
     c = 128**-0.5 * LOG2E
     rows = q.shape[3]
     for e in range(q.shape[1]):
-        s = lax.dot_general(q[0, e, 0], kv[0, e, 0], (((1,), (1,)), ((), ())), preferred_element_type=F32) * c
-        top = jnp.max(s, axis=-1, keepdims=True)
+        s = lax.dot_general(kv[0, e, 0], q[0, e, 0], CONTRACT, preferred_element_type=F32) * c
+        top = jnp.max(s, axis=0, keepdims=True)
         w = jnp.exp2(s - top)
-        total = jnp.sum(w, axis=-1, keepdims=True)
-        o = jnp.dot(w.astype(BF16), kv[0, e, 1], preferred_element_type=F32)
-        out[0, e, 0:rows, :] = (o / total).astype(BF16)
-        lse = jnp.transpose(jnp.broadcast_to(top + jnp.log2(total), (rows, 128)))[0:8, :]
+        total = jnp.sum(w, axis=0, keepdims=True)
+        o = jnp.dot(side_by_side(kv, (0, e, 1)), w.astype(BF16), preferred_element_type=F32)
+        out[0, e, 0:128, :] = (o / total).astype(BF16)
+        lse = jnp.broadcast_to(top + jnp.log2(total), (16, rows))
         first = lse.astype(BF16).astype(F32)
         second = (lse - first).astype(BF16).astype(F32)
         third = lse - first - second
         at = lax.broadcasted_iota(jnp.int32, lse.shape, 0)
-        pieces = jnp.where(at == 0, first, jnp.where(at == 1, second, third))
-        pieces = jnp.concatenate([pieces[:, i : i + 128] for i in range(0, rows, 128)], 0)
-        out[0, e, rows : rows + rows // 16, :] = pieces.astype(BF16)
+        out[0, e, 128:144, :] = jnp.where(at == 0, first, jnp.where(at == 1, second, third)).astype(BF16)
 
 
 def diag(send, fresh):
     prompts, heads, _, rows, _ = fresh.shape
-    tall = rows + rows // 16
-    per = heads
     return pl.pallas_call(
         diag_body,
         grid=(prompts,),
         in_specs=[
-            pl.BlockSpec((1, per, 1, rows, 128), lambda p: (p, 0, 0, 0, 0)),
-            pl.BlockSpec((1, per, 2, rows, 128), lambda p: (p, 0, 0, 0, 0)),
+            pl.BlockSpec((1, heads, 1, rows, 128), lambda p: (p, 0, 0, 0, 0)),
+            pl.BlockSpec((1, heads, 2, rows, 128), lambda p: (p, 0, 0, 0, 0)),
         ],
-        out_specs=pl.BlockSpec((1, SLOTS, tall, 128), lambda p: (p, 0, 0, 0)),
-        out_shape=jax.ShapeDtypeStruct((prompts, SLOTS, tall, 128), BF16),
+        out_specs=pl.BlockSpec((1, SLOTS, 144, rows), lambda p: (p, 0, 0, 0)),
+        out_shape=jax.ShapeDtypeStruct((prompts, SLOTS, 144, rows), BF16),
         compiler_params=pltpu.CompilerParams(
-            dimension_semantics=("arbitrary",), vmem_limit_bytes=VMEM
+            dimension_semantics=("arbitrary",), vmem_limit_bytes=16 * MIB
         ),
         cost_estimate=pl.CostEstimate(
             flops=4 * prompts * heads * rows * rows * 128,
@@ -194,40 +200,48 @@
     )(send, fresh)
 
 
-def attend_body(info, got, text, out, stat, s_even, s_odd, top_s):
+def attend_body(info, got, text_k, text_v, out, stat, s_even, s_odd, top_s):
     g = pl.program_id(0)
     blocks, _, rows, _ = got.shape
     c = 128**-0.5 * LOG2E
-    txt = text.shape[1]
-    lead = txt // rows
+    lead = text_k.shape[0] // rows
     tiles = lead + blocks - 1
-    contract = (((1,), (1,)), ((), ()))
-
-    def keys(b, i, which):
-        if i < lead:
-            return text[which, i * rows : (i + 1) * rows, :]
-        return got[lax.rem(b + 1 + (i - lead), blocks), 1 + which]
-
-    def score(b, i, top, s_ref):
-        s = lax.dot_general(got[b, 0], keys(b, i, 0), contract, preferred_element_type=F32)
-        if i < lead:
-            at = i * rows + lax.broadcasted_iota(jnp.int32, s.shape, 1)
-            s = jnp.where(at < info[0], s, NEG)
-        s_ref[i] = s
-        for e in range(rows // 128):
-            part = s[:, e * 128 : (e + 1) * 128]
+    groups = [list(range(i, min(i + 4, tiles))) for i in range(0, tiles, 4)]
+    if len(groups[-1]) == 1:
+        last = groups.pop()
+        groups[-1] = groups[-1] + last
+
+    def block_of(b, i):
+        return lax.rem(b + 1 + (i - lead), blocks)
+
+    def keys(b, i):
+        return text_k[i * rows : (i + 1) * rows, :] if i < lead else got[block_of(b, i), 1]
+
+    def values(b, i):
+        return text_v[:, i * rows : (i + 1) * rows] if i < lead else side_by_side(got, (block_of(b, i), 2))
+
+    def score(b, group, top, s_ref):
+        k = jnp.concatenate([keys(b, i) for i in group], 0)
+        scores = lax.dot_general(k, got[b, 0], CONTRACT, preferred_element_type=F32)
+        for m, i in enumerate(group):
+            s = scores[m * rows : (m + 1) * rows, :]
+            if i < lead:
+                at = i * rows + lax.broadcasted_iota(jnp.int32, s.shape, 0)
+                s = jnp.where(at < info[0], s, NEG)
+            s_ref[i] = s
+            part = jnp.max(s.reshape(rows // 8, 8, rows), axis=0)
             top = part if top is None else jnp.maximum(top, part)
         return top
 
-    def lane_top(top):
-        return jnp.broadcast_to(jnp.max(top, axis=-1, keepdims=True) * c, (rows, 128))
+    def whole_top(top):
+        return jnp.broadcast_to(jnp.max(top, axis=0, keepdims=True) * c, (8, rows))
 
     @pl.when(g == 0)
     def _():
         top = None
-        for i in range(tiles):
-            top = score(0, i, top, s_even)
-        top_s[...] = lane_top(top)
+        for group in groups:
+            top = score(0, group, top, s_even)
+        top_s[...] = whole_top(top)
 
     top = top_s[...]
     for k in range(2):
@@ -237,28 +251,28 @@
         total = None
         acc = None
         nxt_top = None
-        for i in range(tiles):
-            nxt_top = score(nxt, i, nxt_top, there)
-            s = here[i]
+        for group in groups:
+            nxt_top = score(nxt, group, nxt_top, there)
             w = []
-            for e in range(rows // 128):
-                part = jnp.exp2(s[:, e * 128 : (e + 1) * 128] * c - top)
+            for i in group:
+                x = jnp.exp2(here[i] * c - top[0:1, :])
+                part = jnp.sum(x.reshape(rows // 8, 8, rows), axis=0)
                 total = part if total is None else total + part
-                w.append(part.astype(BF16))
-            o = jnp.dot(jnp.concatenate(w, 1), keys(b, i, 1), preferred_element_type=F32)
+                w.append(x.astype(BF16))
+            v = jnp.concatenate([values(b, i) for i in group], 1)
+            o = jnp.dot(v, jnp.concatenate(w, 0), preferred_element_type=F32)
             acc = o if acc is None else acc + o
-        total = jnp.sum(total, axis=-1, keepdims=True)
         out[k] = acc
-        lane = lax.broadcasted_iota(jnp.int32, (rows, 128), 1)
-        stat[k] = jnp.where(lane < 64, top, total)
-        top = lane_top(nxt_top)
+        total = jnp.broadcast_to(jnp.sum(total, axis=0, keepdims=True), (8, rows))
+        at = lax.broadcasted_iota(jnp.int32, (8, rows), 0)
+        stat[k] = jnp.where(at < 4, top, total)
+        top = whole_top(nxt_top)
     top_s[...] = top
 
 
-def attend(info, got, text):
+def attend(info, got, text_k, text_v):
     blocks, _, rows, _ = got.shape
-    txt = text.shape[1]
-    tiles = txt // rows + blocks - 1
+    tiles = text_k.shape[0] // rows + blocks - 1
     return pl.pallas_call(
         attend_body,
         grid_spec=pltpu.PrefetchScalarGridSpec(
@@ -266,24 +280,25 @@
             grid=(blocks // 2,),
             in_specs=[
                 pl.BlockSpec(got.shape, lambda b, s: (0, 0, 0, 0)),
-                pl.BlockSpec(text.shape, lambda b, s: (0, 0, 0)),
+                pl.BlockSpec(text_k.shape, lambda b, s: (0, 0)),
+                pl.BlockSpec(text_v.shape, lambda b, s: (0, 0)),
             ],
             out_specs=[
-                pl.BlockSpec((2, rows, 128), lambda b, s: (b, 0, 0)),
-                pl.BlockSpec((2, rows, 128), lambda b, s: (b, 0, 0)),
+                pl.BlockSpec((2, 128, rows), lambda b, s: (b, 0, 0)),
+                pl.BlockSpec((2, 8, rows), lambda b, s: (b, 0, 0)),
             ],
             scratch_shapes=[
                 pltpu.VMEM((tiles, rows, rows), F32),
                 pltpu.VMEM((tiles, rows, rows), F32),
-                pltpu.VMEM((rows, 128), F32),
+                pltpu.VMEM((8, rows), F32),
             ],
         ),
         out_shape=[
-            jax.ShapeDtypeStruct((blocks, rows, 128), F32),
-            jax.ShapeDtypeStruct((blocks, rows, 128), F32),
+            jax.ShapeDtypeStruct((blocks, 128, rows), F32),
+            jax.ShapeDtypeStruct((blocks, 8, rows), F32),
         ],
         compiler_params=pltpu.CompilerParams(
-            dimension_semantics=("arbitrary",), vmem_limit_bytes=VMEM
+            dimension_semantics=("arbitrary",), vmem_limit_bytes=32 * MIB
         ),
         cost_estimate=pl.CostEstimate(
             flops=4 * blocks * rows * tiles * rows * 128 * 2,
@@ -291,44 +306,39 @@
             transcendentals=blocks * rows * tiles * rows,
         ),
         name="attend",
-    )(info, got, text)
+    )(info, got, text_k, text_v)
 
 
 def join_body(acc, stat, own, out):
-    rows = acc.shape[1]
     for e in range(acc.shape[0]):
-        top = stat[e, :, 0:1]
-        total = stat[e, :, 64:65]
-        pieces = own[e, rows : rows + rows // 16, :].astype(F32)
-        other = []
-        for i in range(0, rows // 16, 8):
-            lse = pieces[i : i + 1] + pieces[i + 1 : i + 2] + pieces[i + 2 : i + 3]
-            other.append(jnp.transpose(jnp.broadcast_to(lse, (128, 128))))
-        other = jnp.concatenate(other, 0)
+        top = stat[e, 0:1, :]
+        total = stat[e, 4:5, :]
+        pieces = own[e, 128:144, :].astype(F32)
+        other = pieces[0:1, :] + pieces[1:2, :] + pieces[2:3, :]
         high = jnp.maximum(other, top)
         u = jnp.exp2(top - high)
         w = jnp.exp2(other - high)
-        o = (acc[e] * u + own[e, 0:rows, :].astype(F32) * w) / (total * u + w)
-        o = o.astype(BF16)
+        o = (acc[e] * u + own[e, 0:128, :].astype(F32) * w) / (total * u + w)
+        o = jnp.transpose(o).astype(BF16)
         out[e, 0] = o
         out[e, 1] = o
 
 
 def join(acc, stat, own):
-    blocks, rows, _ = acc.shape
+    blocks, _, rows = acc.shape
     per = 4
     return pl.pallas_call(
         join_body,
         grid=(blocks // per,),
         in_specs=[
-            pl.BlockSpec((per, rows, 128), lambda b: (b, 0, 0)),
-            pl.BlockSpec((per, rows, 128), lambda b: (b, 0, 0)),
-            pl.BlockSpec((per, own.shape[1], 128), lambda b: (b, 0, 0)),
+            pl.BlockSpec((per, 128, rows), lambda b: (b, 0, 0)),
+            pl.BlockSpec((per, 8, rows), lambda b: (b, 0, 0)),
+            pl.BlockSpec((per, 144, rows), lambda b: (b, 0, 0)),
         ],
         out_specs=pl.BlockSpec((per, 2, rows, 128), lambda b: (b, 0, 0, 0)),
         out_shape=jax.ShapeDtypeStruct((blocks, 2, rows, 128), BF16),
         compiler_params=pltpu.CompilerParams(
-            dimension_semantics=("arbitrary",), vmem_limit_bytes=VMEM
+            dimension_semantics=("arbitrary",), vmem_limit_bytes=16 * MIB
         ),
         name="join",
     )(acc, stat, own)
@@ -381,7 +391,7 @@
         ),
         out_shape=jax.ShapeDtypeStruct((prompts, rows, width), BF16),
         compiler_params=pltpu.CompilerParams(
-            dimension_semantics=("arbitrary",), vmem_limit_bytes=VMEM
+            dimension_semantics=("arbitrary",), vmem_limit_bytes=20 * MIB
         ),
         cost_estimate=pl.CostEstimate(
             flops=4 * prompts * rows * part * width, bytes_accessed=12_000_000, transcendentals=0
@@ -425,7 +435,8 @@
     text = jnp.pad(text, ((0, 0), (0, SLOTS - heads), (0, 0), (0, 0), (0, 0)))
     text = text.reshape(n_seq, 2, t_rows, head_dim)
     text = lax.all_to_all(text, "seq", split_axis=0, concat_axis=0, tiled=True)
-    text = text.transpose(1, 0, 2, 3).reshape(2, n_seq * t_rows, head_dim)
+    text_k = text[:, 0].reshape(n_seq * t_rows, head_dim)
+    text_v = text[:, 1].reshape(n_seq * t_rows, head_dim).T
 
     n_y = n_seq // 4
     y_seat = seat // 4
@@ -441,13 +452,14 @@
     for d in range(1, n_y):
         moved = lax.ppermute(piece, "seq", [(i, (i + 4 * d) % n_seq) for i in range(n_seq)])
         w_y = lax.dynamic_update_slice(w_y, moved[None], ((y_seat - d) % n_y, 0, 0))
+    other_hidden, w_y = lax.optimization_barrier((other_hidden, w_y))
     w_oth = jnp.zeros((n_batch, n_y, share, width_part), BF16)
     w_oth = lax.dynamic_update_slice(w_oth, w_y[None], (batch_seat, 0, 0, 0))
     for d in range(1, n_batch):
         moved = lax.ppermute(w_y, "batch", [(i, (i + d) % n_batch) for i in range(n_batch)])
         w_oth = lax.dynamic_update_slice(w_oth, moved[None], ((batch_seat - d) % n_batch, 0, 0, 0))
     w_oth = w_oth.reshape(channels, width_part)
-    other_hidden, w_oth = lax.optimization_barrier((other_hidden, w_oth))
+    text_k, w_oth = lax.optimization_barrier((text_k, w_oth))
 
     seats = jnp.arange(n_seq, dtype=jnp.int32)
     own_band = jnp.sum(jnp.where(seats == seat, patch_of, 0))
@@ -473,9 +485,9 @@
     own_part = diag(send, fresh)
     unit_prompt = jnp.minimum(seat // SLOTS, prompts - 1)
     length = jnp.sum(jnp.where(jnp.arange(prompts) == unit_prompt, text_len, 0)).astype(jnp.int32)
-    acc, stat = attend(length[None], got, text)
+    acc, stat = attend(length[None], got, text_k, text_v)
     own_part = lax.all_to_all(
-        own_part.reshape(n_seq, -1, head_dim), "seq", split_axis=0, concat_axis=0, tiled=True
+        own_part.reshape(n_seq, -1, rows), "seq", split_axis=0, concat_axis=0, tiled=True
     )
     back = join(acc, stat, own_part)
     back = lax.all_to_all(

time: 213 us -> 203 us (0.953)
  local copies, waits for them, and re-layouts: 10.4 us -> 25.5 us
  waiting for transfers between devices: 88.6 us -> 76.4 us
  Pallas kernels: 69.3 us -> 58 us
    all_to_all x1, waiting for transfers between devices: 33.1 us -> 6.18 us  [per_device(): lax.all_to_all(send.reshape(n_seq, 3, rows, head_dim), 'seq', split_axis=...]
    ppermute x1, waiting for transfers between devices: 0.01 us -> 20.2 us  [per_device(): other_hidden = lax.ppermute(image_hidden, 'head', swap)]
    unnamed x20 -> x48, local copies, waits for them, and re-layouts: 4.64 us -> 15.4 us
    ppermute x3, waiting for transfers between devices: 23.3 us -> 15.4 us  [per_device(): lax.ppermute(w_y, 'batch', [(i, (i + d) % n_batch) for i in range(n_batch)])]
    pallas_call x1, Pallas kernels: 5.32 us -> 0.81 us  [join(): pl.pallas_call(join_body, grid=(blocks // per,), in_specs=[pl.BlockSpec((...]
    pallas_call x1, Pallas kernels: 32.2 us -> 27.8 us  [attend(): pl.pallas_call(attend_body, grid_spec=pltpu.PrefetchScalarGridSpec(num_sc...]
  transfers between devices with their start and end apart: 12 -> 12, of which waited for: 7 -> 7; matrix products, arithmetic and copies ran while one was open for 5% -> 6% of each run, Pallas kernels for 26% -> 25%
where the time goes in v1:
time: 203 us; the launch traced here: 202 us
  waiting for transfers between devices  76.4 us (38%)
  Pallas kernels  58 us (29%)
  starting transfers between devices  35.9 us (18%)
  local copies, waits for them, and re-layouts  25.5 us (13%)
  other arithmetic  5.31 us (3%)
    pallas_call x1, Pallas kernels, attend(): pl.pallas_call(attend_body, grid_spec=pltpu.PrefetchScalarGridSpec(num_sc...  27.8 us
    all_to_all x1, waiting for transfers between devices, per_device(): lax.all_to_all(back.reshape(n_seq * 2, rows, head_dim), ('seq', 'head'),...  27.4 us
    ppermute x1, waiting for transfers between devices, per_device(): other_hidden = lax.ppermute(image_hidden, 'head', swap)  20.2 us
    pallas_call x1, Pallas kernels, qkv(): pl.pallas_call(qkv_body, grid_spec=pltpu.PrefetchScalarGridSpec(num_scala...  17.1 us
    ppermute x3, waiting for transfers between devices, per_device(): lax.ppermute(w_y, 'batch', [(i, (i + d) % n_batch) for i in range(n_batch)])  15.4 us
    unnamed x48, local copies, waits for them, and re-layouts  15.4 us
    all_to_all x1, starting transfers between devices, per_device(): lax.all_to_all(back.reshape(n_seq * 2, rows, head_dim), ('seq', 'head'),...  7.24 us
    ppermute x3, waiting for transfers between devices, per_device(): lax.ppermute(piece, 'seq', [(i, (i + 4 * d) % n_seq) for i in range(n_seq)])  7.16 us
  transfers between devices with their start and end apart: 12, of which 7 were waited for; matrix products, arithmetic and copies ran while one was open for 6% of the time, Pallas kernels for 25%

profile of v1, /device:TPU:0, one launch (start us, length us, event | category | flops | bytes accessed | tf_op | source)
XLA Modules:
  0.0 202.2 jit_solution(12851878067805797343)
XLA Ops:
  0.0 1.1 stack.33
  1.2 1.0 stack.34
  2.3 0.7 pad.4.clone
  3.0 5.7 %all-to-all-start.1 = ((bf16[16,2,32,128]{3,2,1,0:T(8,128)(2,1)}), bf16[16,2,32,128]{3,2,1,0:T(8,128)(2,1)}, u32[]{:S(2)}, u32[]{:S(2)}) async-start(bf16[16,2,32,128]{3,2,1,0:T(8,128)(2,1)} %bitcast.13), calls=%async_computation.1 | async-start | bytes 524288 | tf_op jit(solution)/shard_map/all_to_all | solution.py:437
  8.7 1.6 dynamic_slice.6
  10.3 2.7 %collective-permute-start.1 = (bf16[48,1536]{1,0:T(8,128)(2,1)}, bf16[48,1536]{1,0:T(8,128)(2,1)}, u32[]{:S(2)}, u32[]{:S(2)}) collective-permute-start(bf16[48,1536]{1,0:T(8,128)(2,1)} %dynamic_slice.6), channel_id=1, source_target_pairs={{0,1},{1,0},{2,3},{3,2},{4,5},{5,4},{6,7},{7,6},{8,9},{9,8},{10,11... | collective-permute-start | bytes 442376 | tf_op jit(solution)/shard_map/ppermute | solution.py:449
  13.1 0.8 collective-permute-start
  13.9 0.7 fusion.11
  14.6 0.7 fusion.12
  15.9 1.2 fusion.2
  17.2 0.8 pad_add_fusion.info
  18.0 1.1 pad_maximum_fusion.1.sin
  19.2 3.2 %collective-permute-start.4 = (bf16[48,1536]{1,0:T(8,128)(2,1)}, bf16[48,1536]{1,0:T(8,128)(2,1)S(1)}, u32[]{:S(2)}, u32[]{:S(2)}) collective-permute-start(bf16[48,1536]{1,0:T(8,128)(2,1)} %collective-permute-done.1), channel_id=1, source_target_pairs={{0,24},{2,26},{4,28},{6,30},{8,0},{10,2},{12,4},{14,6},{16,8},{18,... | collective-permute-start | bytes 442376 | tf_op jit(solution)/shard_map/ppermute | solution.py:453
  22.3 0.9 collective-permute-start.3
  23.2 0.9 collective-permute-start.2
  24.1 0.9 bitcast_dynamic-update-slice_fusion.7
  25.0 7.2 %collective-permute-done.2 = bf16[48,1536]{1,0:T(8,128)(2,1)S(1)} collective-permute-done((bf16[48,1536]{1,0:T(8,128)(2,1)}, bf16[48,1536]{1,0:T(8,128)(2,1)S(1)}, u32[]{:S(2)}, u32[]{:S(2)}) %collective-permute-start.2) | collective-permute-done | bytes 147488 | tf_op jit(solution)/shard_map/ppermute | solution.py:453
  32.3 20.2 %collective-permute-done.oth = bf16[2,256,1536]{2,1,0:T(8,128)(2,1)S(1)} collective-permute-done((bf16[2,256,1536]{2,1,0:T(8,128)(2,1)S(1)}, bf16[2,256,1536]{2,1,0:T(8,128)(2,1)S(1)}, u32[]{:S(2)}, u32[]{:S(2)}) %collective-permute-start) | collective-permute-done | bytes 1572896 | tf_op jit(solution)/shard_map/ppermute | solution.py:430
  52.5 17.1 %qkv.1 = (bf16[2,8,3,256,128]{4,3,2,1,0:T(8,128)(2,1)}, bf16[2,6,2,256,128]{4,3,2,1,0:T(8,128)(2,1)S(1)}) custom-call(s32[2]{0:T(128)S(1)} %pad_add_fusion.info, bf16[2,256,1536]{2,1,0:T(8,128)(2,1)S(1)} %copy-done.1, bf16[2,256,1536]{2,1,0:T(8,128)(2,1)S(1)} %collective-permute-done.oth, f32[3,2,3072]{2,1,0:T(2,128)S(1)} %bitcast.35, ...), custom_call_target="tpu_custom_call" | custom-call | flops 7247757312 | bytes 20000000 | tf_op jit(solution)/shard_map/qkv/pallas_call | solution.py:114
  69.7 1.1 copy-done.6
  70.8 5.0 %all-to-all-start = ((bf16[16,3,256,128]{3,2,1,0:T(8,128)(2,1)}), bf16[16,3,256,128]{3,2,1,0:T(8,128)(2,1)}, u32[]{:S(2)}, u32[]{:S(2)}) async-start(bf16[16,3,256,128]{3,2,1,0:T(8,128)(2,1)} %bitcast.11), calls=%async_computation | async-start | bytes 6291456 | tf_op jit(solution)/shard_map/all_to_all | solution.py:482
  76.5 1.9 collective-permute-start.5
  78.5 1.6 fusion.14
  80.1 0.8 copy.21
  80.9 2.1 %collective-permute-start.7 = (bf16[4,48,1536]{2,1,0:T(8,128)(2,1)S(1)}, bf16[4,48,1536]{2,1,0:T(8,128)(2,1)S(1)}, u32[]{:S(2)}, u32[]{:S(2)}) collective-permute-start(bf16[4,48,1536]{2,1,0:T(8,128)(2,1)S(1)} %copy-done.17), channel_id=1, source_target_pairs={{0,96},{32,0},{64,32},{96,64},{1,97},{33,1},{65,33},{97,65},{2,98}... | collective-permute-start | bytes 1769480 | tf_op jit(solution)/shard_map/ppermute | solution.py:459
  83.0 1.9 collective-permute-start.6
  85.1 1.4 copy-done.7
  86.5 5.6 %diag.1 = bf16[2,8,144,256]{3,2,1,0:T(8,128)(2,1)} custom-call(bf16[2,8,3,256,128]{4,3,2,1,0:T(8,128)(2,1)} %get-tuple-element.14.q, bf16[2,6,2,256,128]{4,3,2,1,0:T(8,128)(2,1)S(1)} %copy-done.7), custom_call_target="tpu_custom_call" | custom-call | flops 402653184 | bytes 4000000 | tf_op jit(solution)/shard_map/diag/pallas_call | solution.py:182
  92.1 2.4 %collective-permute-done.5 = bf16[4,48,1536]{2,1,0:T(8,128)(2,1)} collective-permute-done((bf16[4,48,1536]{2,1,0:T(8,128)(2,1)S(1)}, bf16[4,48,1536]{2,1,0:T(8,128)(2,1)}, u32[]{:S(2)}, u32[]{:S(2)}) %collective-permute-start.5) | collective-permute-done | bytes 589856 | tf_op jit(solution)/shard_map/ppermute | solution.py:459
  94.5 1.1 bitcast_dynamic-update-slice_fusion.2
  95.6 12.6 %collective-permute-done.6 = bf16[4,48,1536]{2,1,0:T(8,128)(2,1)S(1)} collective-permute-done((bf16[4,48,1536]{2,1,0:T(8,128)(2,1)S(1)}, bf16[4,48,1536]{2,1,0:T(8,128)(2,1)S(1)}, u32[]{:S(2)}, u32[]{:S(2)}) %collective-permute-start.6) | collective-permute-done | bytes 589856 | tf_op jit(solution)/shard_map/ppermute | solution.py:459
  108.7 6.2 %all-to-all-done.got = bf16[16,3,256,128]{3,2,1,0:T(8,128)(2,1)} async-done(((bf16[16,3,256,128]{3,2,1,0:T(8,128)(2,1)}), bf16[16,3,256,128]{3,2,1,0:T(8,128)(2,1)}, u32[]{:S(2)}, u32[]{:S(2)}) %all-to-all-start) | async-done | bytes 3145760 | tf_op jit(solution)/shard_map/all_to_all | solution.py:482
  114.9 3.7 %all-to-all-start.2 = ((bf16[16,144,256]{2,1,0:T(8,128)(2,1)}), bf16[16,144,256]{2,1,0:T(8,128)(2,1)S(1)}, u32[]{:S(2)}, u32[]{:S(2)}) async-start(bf16[16,144,256]{2,1,0:T(8,128)(2,1)} %bitcast.22), calls=%async_computation.2 | async-start | bytes 2359296 | tf_op jit(solution)/shard_map/all_to_all | solution.py:489
  118.6 0.9 copy-done.14
  119.5 0.9 copy-done.15
  120.4 27.8 %attend.1 = (f32[16,128,256]{2,1,0:T(8,128)S(1)}, f32[16,8,256]{2,1,0:T(8,128)S(1)}) custom-call(s32[1]{0:T(128)} %bitcast.2.info, bf16[16,3,256,128]{3,2,1,0:T(8,128)(2,1)} %all-to-all-done.got, bf16[512,128]{1,0:T(8,128)(2,1)S(1)} %bitcast.38, bf16[128,512]{1,0:T(8,128)(2,1)S(1)} %bitcast.37), custom_call_target="tpu_custom_call" | custom-call | flops 18253611008 | bytes 8000000 | tf_op jit(solution)/shard_map/attend/pallas_call | solution.py:276
  148.2 1.3 copy-done.4
  150.2 1.6 copy-done.5
  151.8 0.9 copy-done.13
  152.7 0.8 join.1
  153.5 1.3 copy-done
  154.9 7.2 %all-to-all-start.3 = ((bf16[32,256,128]{2,1,0:T(8,128)(2,1)}), bf16[32,256,128]{2,1,0:T(8,128)(2,1)}, u32[]{:S(2)}, u32[]{:S(2)}) async-start(bf16[32,256,128]{2,1,0:T(8,128)(2,1)} %bitcast.34), calls=%async_computation.3 | async-start | bytes 4194304 | tf_op jit(solution)/shard_map/all_to_all | solution.py:493
  162.1 0.7 slice.11
  162.9 27.4 %all-to-all-done.3.got = bf16[32,256,128]{2,1,0:T(8,128)(2,1)} async-done(((bf16[32,256,128]{2,1,0:T(8,128)(2,1)}), bf16[32,256,128]{2,1,0:T(8,128)(2,1)}, u32[]{:S(2)}, u32[]{:S(2)}) %all-to-all-start.3) | async-done | bytes 2097184 | tf_op jit(solution)/shard_map/all_to_all | solution.py:493
  190.2 1.4 copy-done.2
  191.6 2.3 %copy-done.3 = bf16[768,3072]{1,0:T(8,128)(2,1)S(1)} copy-done((bf16[768,3072]{1,0:T(8,128)(2,1)S(1)}, bf16[768,3072]{1,0:T(8,128)(2,1)}, u32[]{:S(2)}) %copy-start.3) | copy-done | bytes 4718616
  194.0 1.4 copy-done.8
  195.4 6.8 %project.1 = bf16[2,256,1536]{2,1,0:T(8,128)(2,1)} custom-call(s32[2]{0:T(128)S(1)} %pad_add_fusion.info, bf16[32,256,128]{2,1,0:T(8,128)(2,1)} %all-to-all-done.3.got, bf16[768,3072]{1,0:T(8,128)(2,1)S(1)} %copy-done.3, bf16[768,1536]{1,0:T(8,128)(2,1)S(1)} %bitcast.33, f32[2,1,1536]{2,1,0:T(1,128)S(1)} %copy.23.gate, bf16[2,256,1536]{2,1,0:T(8,128)(2,1)S(1)} %copy-done.2, ...), custom_call_target="tpu_custom_call" | custom-call | flops 2415919104 | bytes 12000000 | tf_op jit(solution)/shard_map/project/pallas_call | solution.py:376
  (59 shorter events, 2.5 us)
Async XLA Ops:
  0.0 13.1 %copy-start.1 = (bf16[2,256,1536]{2,1,0:T(8,128)(2,1)S(1)}, bf16[2,256,1536]{2,1,0:T(8,128)(2,1)}, u32[]{:S(2)}) copy-start(bf16[2,256,1536]{2,1,0:T(8,128)(2,1)} %hidden.1) | copy-start | bytes 4718596
  0.0 13.9 %copy-start.20 = (s32[16]{0:T(128)S(1)}, s32[16]{0:T(128)}, u32[]{:S(2)}) copy-start(s32[16]{0:T(128)} %param.26) | copy-start | bytes 196
  0.0 14.6 %copy-start.21 = (s32[16]{0:T(128)S(1)}, s32[16]{0:T(128)}, u32[]{:S(2)}) copy-start(s32[16]{0:T(128)} %param.25) | copy-start | bytes 196
  0.0 17.2 %copy-start.18 = (f32[128]{0:T(128)S(1)}, f32[128]{0:T(128)}, u32[]{:S(2)}) copy-start(f32[128]{0:T(128)} %param.19) | copy-start | bytes 1540
  0.0 17.2 %copy-start.19 = (f32[128]{0:T(128)S(1)}, f32[128]{0:T(128)}, u32[]{:S(2)}) copy-start(f32[128]{0:T(128)} %param.18) | copy-start | bytes 1540
  2.3 50.3 %copy-start.11 = (f32[2,3,3072]{2,0,1:T(2,128)S(1)}, f32[2,3,3072]{2,0,1:T(2,128)}, u32[]{:S(2)}) copy-start(f32[2,3,3072]{2,0,1:T(2,128)} %param.15) | copy-start | bytes 221188
  3.0 67.8 %all-to-all-start.1 = ((bf16[16,2,32,128]{3,2,1,0:T(8,128)(2,1)}), bf16[16,2,32,128]{3,2,1,0:T(8,128)(2,1)}, u32[]{:S(2)}, u32[]{:S(2)}) async-start(bf16[16,2,32,128]{3,2,1,0:T(8,128)(2,1)} %bitcast.13), calls=%async_computation.1 | async-start | bytes 524288 | tf_op jit(solution)/shard_map/all_to_all | solution.py:437
  10.3 8.8 %collective-permute-start.1 = (bf16[48,1536]{1,0:T(8,128)(2,1)}, bf16[48,1536]{1,0:T(8,128)(2,1)}, u32[]{:S(2)}, u32[]{:S(2)}) collective-permute-start(bf16[48,1536]{1,0:T(8,128)(2,1)} %dynamic_slice.6), channel_id=1, source_target_pairs={{0,1},{1,0},{2,3},{3,2},{4,5},{5,4},{6,7},{7,6},{8,9},{9,8},{10,11... | collective-permute-start | bytes 442376 | tf_op jit(solution)/shard_map/ppermute | solution.py:449
  13.1 39.5 %collective-permute-start = (bf16[2,256,1536]{2,1,0:T(8,128)(2,1)S(1)}, bf16[2,256,1536]{2,1,0:T(8,128)(2,1)S(1)}, u32[]{:S(2)}, u32[]{:S(2)}) collective-permute-start(bf16[2,256,1536]{2,1,0:T(8,128)(2,1)S(1)} %copy-done.1), channel_id=1, source_target_pairs={{0,1},{1,0},{2,3},{3,2},{4,5},{5,4},{6,7},{7,6},{8,9},{9,8},{10,11... | collective-permute-start | bytes 4718600 | tf_op jit(solution)/shard_map/ppermute | solution.py:430
  18.0 34.5 %copy-start.9 = (bf16[2,256,768]{2,1,0:T(8,128)(2,1)S(1)}, bf16[2,256,768]{2,1,0:T(8,128)(2,1)}, u32[]{:S(2)}) copy-start(bf16[2,256,768]{2,1,0:T(8,128)(2,1)} %stale_k.1) | copy-start | bytes 2359300
  18.0 34.5 %copy-start.10 = (bf16[2,256,768]{2,1,0:T(8,128)(2,1)S(1)}, bf16[2,256,768]{2,1,0:T(8,128)(2,1)}, u32[]{:S(2)}) copy-start(bf16[2,256,768]{2,1,0:T(8,128)(2,1)} %stale_v.1) | copy-start | bytes 2359300
  19.2 13.1 %collective-permute-start.4 = (bf16[48,1536]{1,0:T(8,128)(2,1)}, bf16[48,1536]{1,0:T(8,128)(2,1)S(1)}, u32[]{:S(2)}, u32[]{:S(2)}) collective-permute-start(bf16[48,1536]{1,0:T(8,128)(2,1)} %collective-permute-done.1), channel_id=1, source_target_pairs={{0,24},{2,26},{4,28},{6,30},{8,0},{10,2},{12,4},{14,6},{16,8},{18,... | collective-permute-start | bytes 442376 | tf_op jit(solution)/shard_map/ppermute | solution.py:453
  22.3 9.9 %collective-permute-start.3 = (bf16[48,1536]{1,0:T(8,128)(2,1)}, bf16[48,1536]{1,0:T(8,128)(2,1)S(1)}, u32[]{:S(2)}, u32[]{:S(2)}) collective-permute-start(bf16[48,1536]{1,0:T(8,128)(2,1)} %collective-permute-done.1), channel_id=1, source_target_pairs={{0,16},{2,18},{4,20},{6,22},{8,24},{10,26},{12,28},{14,30},{16,0},... | collective-permute-start | bytes 442376 | tf_op jit(solution)/shard_map/ppermute | solution.py:453
  23.2 9.0 %collective-permute-start.2 = (bf16[48,1536]{1,0:T(8,128)(2,1)}, bf16[48,1536]{1,0:T(8,128)(2,1)S(1)}, u32[]{:S(2)}, u32[]{:S(2)}) collective-permute-start(bf16[48,1536]{1,0:T(8,128)(2,1)} %collective-permute-done.1), channel_id=1, source_target_pairs={{0,8},{2,10},{4,12},{6,14},{8,16},{10,18},{12,20},{14,22},{16,24},... | collective-permute-start | bytes 442376 | tf_op jit(solution)/shard_map/ppermute | solution.py:453
  32.3 20.2 %copy-start.16 = (bf16[4,48,1536]{2,1,0:T(8,128)(2,1)}, bf16[4,48,1536]{2,1,0:T(8,128)(2,1)S(1)}, u32[]{:S(2)}) copy-start(bf16[4,48,1536]{2,1,0:T(8,128)(2,1)S(1)} %bitcast_dynamic-update-slice_fusion.4) | copy-start | bytes 1769476
  69.7 1.1 copy-start.6
  70.8 5.1 %copy-start.22 = (s32[2]{0:T(128)S(1)}, s32[2]{0:T(128)}, u32[]{:S(2)}) copy-start(s32[2]{0:T(128)} %param.27) | copy-start | bytes 28
  70.8 5.7 %copy-start.17 = (bf16[4,48,1536]{2,1,0:T(8,128)(2,1)S(1)}, bf16[4,48,1536]{2,1,0:T(8,128)(2,1)}, u32[]{:S(2)}) copy-start(bf16[4,48,1536]{2,1,0:T(8,128)(2,1)} %copy-done.16) | copy-start | bytes 1769476
  70.8 44.1 %all-to-all-start = ((bf16[16,3,256,128]{3,2,1,0:T(8,128)(2,1)}), bf16[16,3,256,128]{3,2,1,0:T(8,128)(2,1)}, u32[]{:S(2)}, u32[]{:S(2)}) async-start(bf16[16,3,256,128]{3,2,1,0:T(8,128)(2,1)} %bitcast.11), calls=%async_computation | async-start | bytes 6291456 | tf_op jit(solution)/shard_map/all_to_all | solution.py:482
  76.5 17.9 %collective-permute-start.5 = (bf16[4,48,1536]{2,1,0:T(8,128)(2,1)S(1)}, bf16[4,48,1536]{2,1,0:T(8,128)(2,1)}, u32[]{:S(2)}, u32[]{:S(2)}) collective-permute-start(bf16[4,48,1536]{2,1,0:T(8,128)(2,1)S(1)} %copy-done.17), channel_id=1, source_target_pairs={{0,32},{32,64},{64,96},{96,0},{1,33},{33,65},{65,97},{97,1},{2,34}... | collective-permute-start | bytes 1769480 | tf_op jit(solution)/shard_map/ppermute | solution.py:459
  80.9 27.8 %collective-permute-start.7 = (bf16[4,48,1536]{2,1,0:T(8,128)(2,1)S(1)}, bf16[4,48,1536]{2,1,0:T(8,128)(2,1)S(1)}, u32[]{:S(2)}, u32[]{:S(2)}) collective-permute-start(bf16[4,48,1536]{2,1,0:T(8,128)(2,1)S(1)} %copy-done.17), channel_id=1, source_target_pairs={{0,96},{32,0},{64,32},{96,64},{1,97},{33,1},{65,33},{97,65},{2,98}... | collective-permute-start | bytes 1769480 | tf_op jit(solution)/shard_map/ppermute | solution.py:459
  83.0 25.2 %collective-permute-start.6 = (bf16[4,48,1536]{2,1,0:T(8,128)(2,1)S(1)}, bf16[4,48,1536]{2,1,0:T(8,128)(2,1)S(1)}, u32[]{:S(2)}, u32[]{:S(2)}) collective-permute-start(bf16[4,48,1536]{2,1,0:T(8,128)(2,1)S(1)} %copy-done.17), channel_id=1, source_target_pairs={{0,64},{32,96},{64,0},{96,32},{1,65},{33,97},{65,1},{97,33},{2,66}... | collective-permute-start | bytes 1769480 | tf_op jit(solution)/shard_map/ppermute | solution.py:459
  85.1 1.4 copy-start.7
  114.9 35.3 %all-to-all-start.2 = ((bf16[16,144,256]{2,1,0:T(8,128)(2,1)}), bf16[16,144,256]{2,1,0:T(8,128)(2,1)S(1)}, u32[]{:S(2)}, u32[]{:S(2)}) async-start(bf16[16,144,256]{2,1,0:T(8,128)(2,1)} %bitcast.22), calls=%async_computation.2 | async-start | bytes 2359296 | tf_op jit(solution)/shard_map/all_to_all | solution.py:489
  118.6 0.9 copy-start.14
  119.5 0.9 copy-start.15
  148.2 1.3 copy-start.4
  149.6 0.6 copy-start.12
  150.2 1.6 copy-start.5
  151.8 0.9 copy-start.13
  153.5 1.3 copy-start
  154.9 35.4 %all-to-all-start.3 = ((bf16[32,256,128]{2,1,0:T(8,128)(2,1)}), bf16[32,256,128]{2,1,0:T(8,128)(2,1)}, u32[]{:S(2)}, u32[]{:S(2)}) async-start(bf16[32,256,128]{2,1,0:T(8,128)(2,1)} %bitcast.34), calls=%async_computation.3 | async-start | bytes 4194304 | tf_op jit(solution)/shard_map/all_to_all | solution.py:493
  190.2 1.4 copy-start.2
  191.6 2.3 %copy-start.3 = (bf16[768,3072]{1,0:T(8,128)(2,1)S(1)}, bf16[768,3072]{1,0:T(8,128)(2,1)}, u32[]{:S(2)}) copy-start(bf16[768,3072]{1,0:T(8,128)(2,1)} %w_own.1) | copy-start | bytes 14155780
  194.0 1.4 copy-start.8
